TPU v7x, 32 devices: a whole 2x2x4 slice. The times are simulated.
32 devices in a mesh: pts: 4 (over y, core), dir: 4 (over z), freq: 2 (over x).
Axes of the slice: x: 2, y: 2, z: 4, core: 2. Of those that a mesh axis runs over, the one named last changes fastest.
Arguments:
- action: float32 [48, 64, 16384], P('freq', 'dir', 'pts'), may hold values from 0.05 to 2
- bathymetry: float32 [16384], P('pts'), may hold values from 20 to 60
- refraction: float32 [48, 16384], P('freq', 'pts'), may hold values from 0.5 to 2
- shifting: float32 [48, 16384], P('freq', 'pts'), may hold values from 0.5 to 2
- heading: float32 [16384], P('pts'), may hold values from -3.140625 to 3.140625
- slope_angle: float32 [16384], P('pts'), may hold values from -3.140625 to 3.140625
- wet_mask: int32 [16384], P('pts'), may hold values 0 or 1
- substeps: int32 [32], P('pts'), may hold values from 1 to 4
Outputs:
- evolved: float32 [48, 64, 16384], P('freq', 'dir', 'pts')
All inputs are finite; a program needn't handle non-finite values. Where the computation divides by a largest or mean magnitude, that divisor is 1e-20 or more. No bound on the sum of `wet_mask` on one device may be relied on, other than what follows from the above.
Results may differ from a plain program's by a relative error of at most 0.00002.
Values sent between devices are 32-bit elements; how exact they have to be, the bound alone decides.
A program may use at most 64 MiB of HBM per device.

v0:
```python
import functools
import math

import jax
import jax.numpy as jnp
from jax import lax
from jax.experimental import pallas as pl
from jax.experimental.pallas import tpu as pltpu
from jax.sharding import PartitionSpec as P

FREQ = 48
DIR = 64
KMAX = 4
BLK = 512
CHUNK = 256
HALO = KMAX
SUB = 8

EPSILON = 1e-06
MESH = pl.DeviceIdType.MESH


def kernel(
    n_pts,
    n_dir,
    n_freq,
    action_ref,
    head_ref,
    tail_ref,
    depth_ref,
    refraction_ref,
    shifting_ref,
    heading_ref,
    slope_ref,
    wet_ref,
    count_ref,
    out_ref,
    own,
    upper,
    lower,
    ext,
    shext,
    face_shift,
    turn_row,
    shift_row,
    trig,
    depth_in,
    peaks,
    own_sem,
    dir_send,
    dir_recv,
    freq_send,
    freq_recv,
    sh_send,
    sh_recv,
    depth_send,
    depth_recv,
    peak_send,
    peak_recv,
):
    freq_local, dir_local, points = own.shape
    chunks = points // CHUNK
    rows = -(-(dir_local + 2 * HALO) // SUB) * SUB
    pts_at = lax.axis_index("pts")
    dir_at = lax.axis_index("dir")
    freq_at = lax.axis_index("freq")
    dir_up, dir_down = lax.rem(dir_at + 1, n_dir), lax.rem(dir_at + n_dir - 1, n_dir)
    pts_up, pts_down = lax.rem(pts_at + 1, n_pts), lax.rem(pts_at + n_pts - 1, n_pts)
    group = n_pts * n_freq
    member = pts_at * n_freq + freq_at
    has_above = freq_at < n_freq - 1
    has_below = freq_at > 0

    def peer(offset):
        other = lax.rem(member + offset, group)
        return {"pts": other // n_freq, "freq": lax.rem(other, n_freq)}

    barrier = pltpu.get_barrier_semaphore()
    for target in (dir_up, dir_down):
        pl.semaphore_signal(barrier, inc=1, device_id={"dir": target}, device_id_type=MESH)
    for offset in range(1, group):
        pl.semaphore_signal(barrier, inc=1, device_id=peer(offset), device_id_type=MESH)
    pl.semaphore_wait(barrier, 2 + group - 1)

    def span(c):
        return pl.ds(pl.multiple_of(c * CHUNK, CHUNK), CHUNK)

    def remote(src, dst, send, recv, where):
        return pltpu.make_async_remote_copy(
            src_ref=src, dst_ref=dst, send_sem=send, recv_sem=recv, device_id=where, device_id_type=MESH
        )

    def depth_copies():
        return (
            remote(
                depth_ref.at[:, pl.ds(points - 128, 128)],
                depth_in.at[0],
                depth_send.at[0],
                depth_recv.at[0],
                {"pts": pts_up},
            ),
            remote(
                depth_ref.at[:, pl.ds(0, 128)],
                depth_in.at[1],
                depth_send.at[1],
                depth_recv.at[1],
                {"pts": pts_down},
            ),
        )

    def dir_copies(c):
        return (
            remote(
                tail_ref.at[:, :, span(c)],
                lower.at[:, :, span(c)],
                dir_send.at[0, c],
                dir_recv.at[0, c],
                {"dir": dir_up},
            ),
            remote(
                head_ref.at[:, :, span(c)],
                upper.at[:, :, span(c)],
                dir_send.at[1, c],
                dir_recv.at[1, c],
                {"dir": dir_down},
            ),
        )

    def own_copy(c):
        return pltpu.make_async_copy(action_ref.at[:, :, span(c)], own.at[:, :, span(c)], own_sem.at[c])

    above, below = lax.rem(freq_at + 1, n_freq), lax.rem(freq_at + n_freq - 1, n_freq)

    def rise(src, dst, send, recv):
        return remote(src, dst, send, recv, {"freq": above})

    def fall(src, dst, send, recv):
        return remote(src, dst, send, recv, {"freq": below})

    def freq_copies(c):
        return (
            rise(
                ext.at[pl.ds(freq_local, HALO), :, span(c)],
                ext.at[pl.ds(0, HALO), :, span(c)],
                freq_send.at[0, c],
                freq_recv.at[0, c],
            ),
            fall(
                ext.at[pl.ds(HALO, HALO), :, span(c)],
                ext.at[pl.ds(freq_local + HALO, HALO), :, span(c)],
                freq_send.at[1, c],
                freq_recv.at[1, c],
            ),
        )

    def sh_copies():
        return (
            rise(
                shifting_ref.at[pl.ds(freq_local - SUB, SUB)],
                shext.at[0],
                sh_send.at[0],
                sh_recv.at[0],
            ),
            fall(shifting_ref.at[pl.ds(0, SUB)], shext.at[1], sh_send.at[1], sh_recv.at[1]),
        )

    def start_pair(pair):
        @pl.when(has_above)
        def _():
            pair[0].start()

        @pl.when(has_below)
        def _():
            pair[1].start()

    def wait_pair(pair):
        @pl.when(has_above)
        def _():
            pair[0].wait_send()
            pair[1].wait_recv()

        @pl.when(has_below)
        def _():
            pair[1].wait_send()
            pair[0].wait_recv()

    for copy in depth_copies():
        copy.start()

    @pl.loop(0, chunks)
    def _(c):
        for copy in dir_copies(c):
            copy.start()
        own_copy(c).start()

    start_pair(sh_copies())

    row = lax.broadcasted_iota(jnp.int32, (rows, CHUNK), 0)
    offset = jnp.where(row >= rows - HALO, row - rows, row)
    angle = ((dir_at * dir_local + offset).astype(jnp.float32) + 0.5) * (2.0 * math.pi / DIR)
    trig[0] = jnp.sin(angle)
    trig[1] = jnp.cos(angle)
    half = lax.broadcasted_iota(jnp.int32, (DIR // 2, 128), 0)
    half_angle = (half.astype(jnp.float32) + 0.5) * (2.0 * math.pi / DIR)
    half_sin, half_cos = jnp.sin(half_angle), jnp.cos(half_angle)
    wet = wet_ref[...].astype(jnp.float32)
    trig_row = (jnp.sin(slope_ref[...]), jnp.cos(slope_ref[...]), jnp.sin(heading_ref[...]), jnp.cos(heading_ref[...]))
    turn_row[1:2, :] = trig_row[0]
    turn_row[2:3, :] = trig_row[1]
    shift_row[1:2, :] = trig_row[2]
    shift_row[2:3, :] = trig_row[3]

    @pl.when(jnp.logical_not(has_below))
    def _():
        @pl.loop(0, HALO)
        def _(f):
            ext[f] = jnp.zeros((dir_local, points), jnp.float32)

    @pl.when(jnp.logical_not(has_above))
    def _():
        @pl.loop(freq_local + HALO, freq_local + 2 * HALO)
        def _(f):
            ext[f] = jnp.zeros((dir_local, points), jnp.float32)

    for copy in depth_copies():
        copy.wait()
    depth = depth_ref[...]
    lane = lax.broadcasted_iota(jnp.int32, (1, points), 1)
    before = jnp.where(pts_at == 0, depth[:, :1], depth_in[0][:, 127:128])
    after = jnp.where(pts_at == n_pts - 1, depth[:, points - 1 :], depth_in[1][:, :1])
    left = jnp.where(lane == 0, before, pltpu.roll(depth, 1, 1))
    right = jnp.where(lane == points - 1, after, pltpu.roll(depth, points - 1, 1))
    slope = (right - left) * 0.5 * wet
    turn_row[0:1, :] = slope
    shift_row[0:1, :] = wet

    def peak_step(i, carry):
        turn, shift = carry
        part = pl.ds(pl.multiple_of(i * 128, 128), 128)
        sines = jnp.abs(half_sin * turn_row[2:3, part] - half_cos * turn_row[1:2, part])
        cosines = jnp.abs(half_cos * shift_row[2:3, part] + half_sin * shift_row[1:2, part])
        turn_peak = jnp.max(sines, axis=0, keepdims=True) * jnp.abs(turn_row[0:1, part])
        shift_peak = jnp.max(cosines, axis=0, keepdims=True) * shift_row[0:1, part]
        turn = jnp.maximum(turn, jnp.abs(refraction_ref[:, part]) * turn_peak)
        shift = jnp.maximum(shift, jnp.abs(shifting_ref[:, part]) * shift_peak)
        return turn, shift

    zero = jnp.zeros((freq_local, 128), jnp.float32)
    turn, shift = lax.fori_loop(0, points // 128, peak_step, (zero, zero))
    turn = jnp.max(jnp.max(turn, axis=0, keepdims=True), axis=1, keepdims=True)
    shift = jnp.max(jnp.max(shift, axis=0, keepdims=True), axis=1, keepdims=True)
    tile = lax.broadcasted_iota(jnp.int32, (SUB, 128), 0)
    peaks[member] = jnp.where(tile < SUB // 2, turn, shift)

    wait_pair(sh_copies())
    face_rows = freq_local + 2 * HALO
    first = freq_at * freq_local - HALO

    @pl.loop(0, points // CHUNK)
    def _(c):
        part = span(c)
        window = jnp.concatenate(
            [shext[0, :, part][SUB - HALO :], shifting_ref[:, part], shext[1, :, part][:HALO]], axis=0
        )
        following = jnp.concatenate([window[1:], window[:1]], axis=0)
        mark = first + lax.broadcasted_iota(jnp.int32, (face_rows, CHUNK), 0)
        valid = (mark >= 0) & (mark + 1 <= FREQ - 1)
        face_shift[:, part] = jnp.where(valid, 0.5 * (window + following), 0.0)

    def peak_copy(offset):
        return remote(
            peaks.at[member], peaks.at[member], peak_send.at[offset], peak_recv.at[offset], peer(offset)
        )

    def peak_arrival(offset):
        source = lax.rem(member + group - offset, group)
        return remote(
            peaks.at[source], peaks.at[source], peak_send.at[offset], peak_recv.at[offset], peer(offset)
        )

    for offset in range(1, group):
        peak_copy(offset).start()
    for offset in range(1, group):
        peak_copy(offset).wait_send()
        peak_arrival(offset).wait_recv()
    top = jnp.max(peaks[...], axis=0)
    scale_turn = 0.5 / (top[0:1, 0:1] + EPSILON)
    scale_shift = 0.5 / (top[SUB // 2 : SUB // 2 + 1, 0:1] + EPSILON)
    count = count_ref[...].astype(jnp.float32)
    turn_row[0:1, :] = turn_row[0:1, :] * scale_turn / count
    shift_row[3:4, :] = shift_row[0:1, :] * scale_shift / count

    def masks(c):
        per_point = count_ref[:, span(c)]
        return [None] + [jnp.where(per_point > k, 1.0, 0.0) for k in range(1, KMAX)]

    def turn_chunk(c):
        part = span(c)
        for copy in dir_copies(c):
            copy.wait()
        own_copy(c).wait()
        speed = (trig[0] * turn_row[2:3, part] - trig[1] * turn_row[1:2, part]) * turn_row[0:1, part]
        face = 0.5 * (speed + pltpu.roll(speed, rows - 1, 0))
        down = jnp.maximum(face, 0.0)
        up = jnp.minimum(face, 0.0)
        active = masks(c)

        def one(f):
            pieces = [own[f, :, part], upper[f, :, part]]
            spare = rows - dir_local - 2 * HALO
            if spare:
                pieces.append(jnp.zeros((spare, CHUNK), jnp.float32))
            pieces.append(lower[f, :, part])
            cells = jnp.concatenate(pieces, axis=0)
            rate = refraction_ref[pl.ds(f, 1), part]
            for k in range(KMAX):
                flux = down * cells + up * pltpu.roll(cells, rows - 1, 0)
                step = rate if k == 0 else rate * active[k]
                cells = cells - step * (flux - pltpu.roll(flux, 1, 0))
            ext[HALO + f, :, part] = cells[:dir_local]

        for f in range(HALO):
            one(f)
            one(freq_local - HALO + f)

        @pl.loop(HALO, freq_local - HALO, step=2)
        def _(f):
            one(f)
            one(f + 1)

        start_pair(freq_copies(c))

    def shift_chunk(c):
        part = span(c)
        wait_pair(freq_copies(c))
        speed = (
            trig[1, :dir_local] * shift_row[2:3, part] + trig[0, :dir_local] * shift_row[1:2, part]
        ) * shift_row[3:4, part]
        high = jnp.maximum(speed, 0.0)
        low = jnp.minimum(speed, 0.0)
        active = masks(c)
        wet_part = shift_row[0:1, part]
        for k in range(KMAX):
            high_k = high if k == 0 else high * active[k]
            low_k = low if k == 0 else low * active[k]

            def flux_at(j, here, there):
                return face_shift[pl.ds(j, 1), part] * (high_k * here + low_k * there)

            here = ext[k + 1, :, part]
            flux = flux_at(k, ext[k, :, part], here)

            def step(j, carry):
                here, flux = carry
                there = ext[j + 1, :, part]
                beyond = flux_at(j, here, there)
                cells = here - (beyond - flux)
                if k == KMAX - 1:
                    out_ref[j - HALO, :, part] = cells * wet_part
                else:
                    ext[j, :, part] = cells
                return there, beyond

            lax.fori_loop(k + 1, freq_local + 2 * HALO - 1 - k, step, (here, flux), unroll=2)

    turn_chunk(0)

    @pl.loop(1, chunks)
    def _(c):
        turn_chunk(c)
        shift_chunk(c - 1)

    shift_chunk(chunks - 1)


def local(mesh, action, bathymetry, refraction, shifting, heading, slope_angle, wet_mask, substeps):
    freq_local, dir_local, points = action.shape
    n_pts, n_dir, n_freq = mesh.shape["pts"], mesh.shape["dir"], mesh.shape["freq"]
    chunks = points // CHUNK
    rows = -(-(dir_local + 2 * HALO) // SUB) * SUB
    group = n_pts * n_freq
    counts = jnp.broadcast_to(substeps[:, None], (substeps.shape[0], BLK)).reshape(1, points)
    vmem = pl.BlockSpec(memory_space=pltpu.VMEM)
    dma = pltpu.SemaphoreType.DMA
    return pl.pallas_call(
        functools.partial(kernel, n_pts, n_dir, n_freq),
        out_shape=jax.ShapeDtypeStruct(action.shape, jnp.float32),
        in_specs=[pl.BlockSpec(memory_space=pl.ANY)] + [vmem] * 9,
        out_specs=vmem,
        scratch_shapes=[
            pltpu.VMEM((freq_local, dir_local, points), jnp.float32),
            pltpu.VMEM((freq_local, HALO, points), jnp.float32),
            pltpu.VMEM((freq_local, HALO, points), jnp.float32),
            pltpu.VMEM((freq_local + 2 * HALO, dir_local, points), jnp.float32),
            pltpu.VMEM((2, SUB, points), jnp.float32),
            pltpu.VMEM((freq_local + 2 * HALO, points), jnp.float32),
            pltpu.VMEM((SUB, points), jnp.float32),
            pltpu.VMEM((SUB, points), jnp.float32),
            pltpu.VMEM((2, rows, CHUNK), jnp.float32),
            pltpu.VMEM((2, 1, 128), jnp.float32),
            pltpu.VMEM((group, SUB, 128), jnp.float32),
            dma((chunks,)),
            dma((2, chunks)),
            dma((2, chunks)),
            dma((2, chunks)),
            dma((2, chunks)),
            dma((2,)),
            dma((2,)),
            dma((2,)),
            dma((2,)),
            dma((group,)),
            dma((group,)),
        ],
        compiler_params=pltpu.CompilerParams(
            collective_id=0, has_side_effects=True, vmem_limit_bytes=60 * 1024 * 1024
        ),
    )(
        action,
        lax.slice_in_dim(action, 0, HALO, axis=1),
        lax.slice_in_dim(action, dir_local - HALO, dir_local, axis=1),
        bathymetry.reshape(1, points),
        refraction,
        shifting,
        heading.reshape(1, points),
        slope_angle.reshape(1, points),
        wet_mask.reshape(1, points),
        counts,
    )


def solution(mesh):
    placed = (
        P("freq", "dir", "pts"),
        P("pts"),
        P("freq", "pts"),
        P("freq", "pts"),
        P("pts"),
        P("pts"),
        P("pts"),
        P("pts"),
    )
    return jax.shard_map(
        functools.partial(local, mesh),
        mesh=mesh,
        in_specs=placed,
        out_specs=P("freq", "dir", "pts"),
        check_vma=False,
    )
```

profile of v0, /device:TPU:0, one launch (start us, length us, event | category | flops | bytes accessed | tf_op | source)
XLA Modules:
  0.0 98.3 jit_solution(11817943703558285136)
XLA Ops:
  0.0 0.0 copy-start
  0.0 0.7 copy-done
  0.7 0.1 broadcast_bitcast_fusion
  0.7 0.6 copy.9
  1.3 5.2 %fusion = (f32[24,4,4096]{2,1,0:T(4,128)}, f32[24,4,4096]{2,1,0:T(4,128)}) fusion(f32[24,16,4096]{2,1,0:T(8,128)} %action_ref.1), kind=kLoop, calls=%fused_computation.1 | loop fusion | bytes 6291456 | tf_op jit(solution)/shard_map/slice | solution.py:420
  6.5 85.6 %shard_map.82 = f32[24,16,4096]{2,1,0:T(8,128)} custom-call(f32[24,16,4096]{2,1,0:T(8,128)} %action_ref.1, f32[24,4,4096]{2,1,0:T(4,128)} %get-tuple-element.6.head_ref, f32[24,4,4096]{2,1,0:T(4,128)} %get-tuple-element.5.tail_ref, f32[1,4096]{1,0:T(1,128)} %bitcast.9, f32[24,4096]{1,0:T(8,128)} %refraction_ref.1, f32[24,4096]{1,0:T(8,128)} %shifting_ref.1, ...), custom_call_target="tpu_custom_call" | custom-call | tf_op jit(solution)/shard_map/pallas_call | solution.py:385
  92.1 6.2 %copy.11 = f32[24,16,4096]{2,1,0:T(8,128)} copy(f32[24,16,4096]{2,1,0:T(8,128)} %shard_map.82) | data formatting | bytes 12582912
Async XLA Ops:
  0.0 0.7 copy-start
where the time goes:
time: 98.4 us; the launch traced here: 98.3 us
  Pallas kernels  85.6 us (87%)
  local copies, waits for them, and re-layouts  12.7 us (13%)
    pallas_call x1, Pallas kernels, local(): pl.pallas_call(functools.partial(kernel, n_pts, n_dir, n_freq), out_shape...  85.6 us
    unnamed x5, local copies, waits for them, and re-layouts  7.54 us
    slice x1, local copies, waits for them, and re-layouts, local(): lax.slice_in_dim(action, dir_local - HALO, dir_local, axis=1)  5.16 us

commit v1 on v0

--- a/solution.py
+++ b/solution.py
@@ -25,15 +25,13 @@
     n_dir,
     n_freq,
     action_ref,
-    head_ref,
-    tail_ref,
     depth_ref,
     refraction_ref,
     shifting_ref,
     heading_ref,
     slope_ref,
     wet_ref,
-    count_ref,
+    substeps_ref,
     out_ref,
     own,
     upper,
@@ -43,6 +41,7 @@
     face_shift,
     turn_row,
     shift_row,
+    count_row,
     trig,
     depth_in,
     peaks,
@@ -111,14 +110,14 @@
     def dir_copies(c):
         return (
             remote(
-                tail_ref.at[:, :, span(c)],
+                action_ref.at[:, pl.ds(dir_local - HALO, HALO), span(c)],
                 lower.at[:, :, span(c)],
                 dir_send.at[0, c],
                 dir_recv.at[0, c],
                 {"dir": dir_up},
             ),
             remote(
-                head_ref.at[:, :, span(c)],
+                action_ref.at[:, pl.ds(0, HALO), span(c)],
                 upper.at[:, :, span(c)],
                 dir_send.at[1, c],
                 dir_recv.at[1, c],
@@ -286,12 +285,17 @@
     top = jnp.max(peaks[...], axis=0)
     scale_turn = 0.5 / (top[0:1, 0:1] + EPSILON)
     scale_shift = 0.5 / (top[SUB // 2 : SUB // 2 + 1, 0:1] + EPSILON)
-    count = count_ref[...].astype(jnp.float32)
+    for block in range(points // BLK):
+        part = pl.ds(block * BLK, BLK)
+        count_row[0:1, part] = jnp.broadcast_to(
+            substeps_ref[0:1, block : block + 1].astype(jnp.float32), (1, BLK)
+        )
+    count = count_row[0:1, :]
     turn_row[0:1, :] = turn_row[0:1, :] * scale_turn / count
     shift_row[3:4, :] = shift_row[0:1, :] * scale_shift / count
 
     def masks(c):
-        per_point = count_ref[:, span(c)]
+        per_point = count_row[0:1, span(c)]
         return [None] + [jnp.where(per_point > k, 1.0, 0.0) for k in range(1, KMAX)]
 
     def turn_chunk(c):
@@ -379,13 +383,12 @@
     chunks = points // CHUNK
     rows = -(-(dir_local + 2 * HALO) // SUB) * SUB
     group = n_pts * n_freq
-    counts = jnp.broadcast_to(substeps[:, None], (substeps.shape[0], BLK)).reshape(1, points)
     vmem = pl.BlockSpec(memory_space=pltpu.VMEM)
     dma = pltpu.SemaphoreType.DMA
     return pl.pallas_call(
         functools.partial(kernel, n_pts, n_dir, n_freq),
         out_shape=jax.ShapeDtypeStruct(action.shape, jnp.float32),
-        in_specs=[pl.BlockSpec(memory_space=pl.ANY)] + [vmem] * 9,
+        in_specs=[pl.BlockSpec(memory_space=pltpu.HBM)] + [vmem] * 7,
         out_specs=vmem,
         scratch_shapes=[
             pltpu.VMEM((freq_local, dir_local, points), jnp.float32),
@@ -394,6 +397,7 @@
             pltpu.VMEM((freq_local + 2 * HALO, dir_local, points), jnp.float32),
             pltpu.VMEM((2, SUB, points), jnp.float32),
             pltpu.VMEM((freq_local + 2 * HALO, points), jnp.float32),
+            pltpu.VMEM((SUB, points), jnp.float32),
             pltpu.VMEM((SUB, points), jnp.float32),
             pltpu.VMEM((SUB, points), jnp.float32),
             pltpu.VMEM((2, rows, CHUNK), jnp.float32),
@@ -412,19 +416,17 @@
             dma((group,)),
         ],
         compiler_params=pltpu.CompilerParams(
-            collective_id=0, has_side_effects=True, vmem_limit_bytes=60 * 1024 * 1024
+            collective_id=0, has_side_effects=True, vmem_limit_bytes=44 * 1024 * 1024
         ),
     )(
         action,
-        lax.slice_in_dim(action, 0, HALO, axis=1),
-        lax.slice_in_dim(action, dir_local - HALO, dir_local, axis=1),
         bathymetry.reshape(1, points),
         refraction,
         shifting,
         heading.reshape(1, points),
         slope_angle.reshape(1, points),
         wet_mask.reshape(1, points),
-        counts,
+        substeps.reshape(1, -1),
     )
 
 

time: 98.4 us -> 89.8 us (0.913)
  Pallas kernels: 85.6 us -> 81 us
  local copies, waits for them, and re-layouts: 12.7 us -> 8.22 us
    slice x1 -> x0, local copies, waits for them, and re-layouts: 5.16 us -> none  [local(): lax.slice_in_dim(action, dir_local - HALO, dir_local, axis=1)]
    pallas_call x1, Pallas kernels: 85.6 us -> 81 us  [local(): pl.pallas_call(functools.partial(kernel, n_pts, n_dir, n_freq), out_shape...]
    unnamed x5 -> x15, local copies, waits for them, and re-layouts: 7.54 us -> 8.22 us
where the time goes in v1:
time: 89.8 us; the launch traced here: 89.2 us
  Pallas kernels  81 us (90%)
  local copies, waits for them, and re-layouts  8.22 us (9%)
    pallas_call x1, Pallas kernels, local(): pl.pallas_call(functools.partial(kernel, n_pts, n_dir, n_freq), out_shape...  81 us
    unnamed x15, local copies, waits for them, and re-layouts  8.22 us

profile of v1, /device:TPU:0, one launch (start us, length us, event | category | flops | bytes accessed | tf_op | source)
XLA Modules:
  0.0 89.2 jit_solution(169305683251071425)
XLA Ops:
  0.0 0.0 copy-start
  0.0 1.0 %copy-done = f32[24,4096]{1,0:T(8,128)S(1)} copy-done((f32[24,4096]{1,0:T(8,128)S(1)}, f32[24,4096]{1,0:T(8,128)}, u32[]{:S(2)}) %copy-start) | copy-done | bytes 393240
  1.0 0.0 copy-start.1
  1.0 1.0 %copy-done.1 = f32[24,4096]{1,0:T(8,128)S(1)} copy-done((f32[24,4096]{1,0:T(8,128)S(1)}, f32[24,4096]{1,0:T(8,128)}, u32[]{:S(2)}) %copy-start.1) | copy-done | bytes 393240
  2.0 0.0 copy-start.2
  2.0 0.7 copy-done.2
  2.7 0.0 copy-start.3
  2.7 0.7 copy-done.3
  3.4 0.0 copy-start.4
  3.4 0.7 copy-done.4
  4.1 0.0 copy-start.5
  4.1 0.7 copy-done.5
  4.9 0.0 copy-start.6
  4.9 0.7 copy-done.6
  5.5 81.0 %shard_map.82 = f32[24,16,4096]{2,1,0:T(8,128)S(1)} custom-call(f32[24,16,4096]{2,1,0:T(8,128)} %action_ref.1, f32[1,4096]{1,0:T(1,128)S(1)} %bitcast.5, f32[24,4096]{1,0:T(8,128)S(1)} %copy-done, f32[24,4096]{1,0:T(8,128)S(1)} %copy-done.1, f32[1,4096]{1,0:T(1,128)S(1)} %bitcast.6, f32[1,4096]{1,0:T(1,128)S(1)} %bitcast.7, s32[1,4096]{1,0:T(1,128)S(1)} %bitcast.8, ...), custom_call_target="tpu_custom_call" | custom-call | tf_op jit(solution)/shard_map/pallas_call | solution.py:388
  86.5 2.7 %copy.10 = f32[24,16,4096]{2,1,0:T(8,128)} copy(f32[24,16,4096]{2,1,0:T(8,128)S(1)} %shard_map.82) | data formatting | bytes 12582912
Async XLA Ops:
  0.0 1.0 %copy-start = (f32[24,4096]{1,0:T(8,128)S(1)}, f32[24,4096]{1,0:T(8,128)}, u32[]{:S(2)}) copy-start(f32[24,4096]{1,0:T(8,128)} %refraction_ref.1) | copy-start | bytes 1179652
  1.0 1.0 %copy-start.1 = (f32[24,4096]{1,0:T(8,128)S(1)}, f32[24,4096]{1,0:T(8,128)}, u32[]{:S(2)}) copy-start(f32[24,4096]{1,0:T(8,128)} %shifting_ref.1) | copy-start | bytes 1179652
  2.0 0.7 copy-start.2
  2.7 0.7 copy-start.3
  3.4 0.7 copy-start.4
  4.1 0.7 copy-start.5
  4.9 0.7 copy-start.6
